TPU v7x, 32 devices: a whole 2x2x4 slice. The times are simulated.
32 devices in a mesh: dp: 16 (over z, y, core), local: 2 (over x).
Axes of the slice: x: 2, y: 2, z: 4, core: 2. Of those that a mesh axis runs over, the one named last changes fastest.
Arguments:
- pre_glu: bfloat16 [32, 256, 3072], P(('dp', 'local')), may hold values from -80 to 80
- lengths: int32 [32], P(('dp', 'local')), may hold values from 1 to 256, as said below
- kernel: float32 [5, 1536], replicated, may hold values from -2.5 to 2.5
- bn_gain: float32 [1536], replicated, may hold values from 0.5 to 2
- bn_shift: float32 [1536], replicated, may hold values from -1 to 1
- w_out: bfloat16 [1536, 1536], replicated, may hold values from -0.15625 to 0.15625
- cotangent: bfloat16 [32, 256, 1536], P(('dp', 'local')), may hold values from -6 to 6
Outputs:
- grad_pre_glu: bfloat16 [32, 256, 3072], P(('dp', 'local'))
- grad_w_out: float32 [1536, 1536], P('dp', 'local')
- grad_kernel: float32 [5, 1536], replicated
- grad_gain: float32 [1536], replicated
- grad_shift: float32 [1536], replicated
Inputs may be any that keep to these rules, and one draw needn't show every extreme that they name: `lengths`: each utterance's valid frames are its first ones; some utterance has all 256 frames valid.
All inputs are finite; a program needn't handle non-finite values.
Results may differ from a plain program's by a relative error of at most 0.0029.
Values sent between devices are 32-bit elements; how exact they have to be, the bound alone decides.
A program may use at most 64 MiB of HBM per device.

v0:
```python
import jax
import jax.numpy as jnp
from jax import lax
from jax.sharding import PartitionSpec as P

epsilon = 1e-05


def on_device(pre_glu, lengths, kernel, bn_gain, bn_shift, w_out, cotangent):
    frames = pre_glu.shape[1]
    model_width = kernel.shape[1]
    kernel_taps = kernel.shape[0]
    half_width = (kernel_taps - 1) // 2
    replicas = lax.axis_size("dp") * lax.axis_size("local")
    valid_mask = (jnp.arange(frames, dtype=jnp.int32)[:, None] < lengths[0]).astype(jnp.float32)
    first_half = pre_glu[0, :, :model_width].astype(jnp.float32)
    gate_value = jax.nn.sigmoid(pre_glu[0, :, model_width:].astype(jnp.float32))
    glu_out = first_half * gate_value * valid_mask
    padded = jnp.pad(glu_out, ((half_width, half_width), (0, 0)))
    conv_out = kernel[0] * padded[0:frames]
    for j in range(1, kernel_taps):
        conv_out = conv_out + kernel[j] * padded[j : j + frames]
    own_count = lengths[0].astype(jnp.float32)
    sum_first, sum_square, frame_total = lax.psum(
        (
            jnp.sum(conv_out * valid_mask, 0),
            jnp.sum(conv_out * conv_out * valid_mask, 0),
            own_count,
        ),
        ("dp", "local"),
    )
    mean_value = sum_first / frame_total
    variance = sum_square / frame_total - mean_value * mean_value
    invstd = lax.rsqrt(variance + epsilon)
    normed = (conv_out - mean_value) * invstd
    act_in = bn_gain * normed + bn_shift
    sig_act = jax.nn.sigmoid(act_in)
    swished = (act_in * sig_act).astype(jnp.bfloat16)
    masked_cot = cotangent[0] * valid_mask.astype(jnp.bfloat16)
    contract = (((0,), (0,)), ((), ()))
    wgrad_term = lax.dot_general(swished, masked_cot, contract, preferred_element_type=jnp.float32)
    partial_value = lax.psum_scatter(wgrad_term, "dp", scatter_dimension=0, tiled=True)
    weight_shard = lax.psum_scatter(partial_value, "local", scatter_dimension=1, tiled=True)
    grad_swish = lax.dot_general(
        masked_cot, w_out, (((1,), (1,)), ((), ())), preferred_element_type=jnp.float32
    )
    grad_act = grad_swish * sig_act * (1.0 + act_in * (1.0 - sig_act))
    channel_scale = bn_gain * invstd
    sum_shift, sum_gain = lax.psum(
        (jnp.sum(grad_act, 0), jnp.sum(grad_act * normed, 0)), ("dp", "local")
    )
    grad_conv = (
        valid_mask * channel_scale * (grad_act - (sum_shift + normed * sum_gain) / frame_total)
    )
    kernel_part = jnp.stack(
        [jnp.sum(grad_conv * padded[j : j + frames], 0) for j in range(kernel_taps)], 0
    )
    kernel_sum = lax.psum(kernel_part, ("dp", "local"))
    grad_padded = jnp.pad(grad_conv, ((half_width, half_width), (0, 0)))
    grad_glu = kernel[0] * grad_padded[kernel_taps - 1 : kernel_taps - 1 + frames]
    for j in range(1, kernel_taps):
        grad_glu = (
            grad_glu + kernel[j] * grad_padded[kernel_taps - 1 - j : kernel_taps - 1 - j + frames]
        )
    grad_glu = grad_glu * valid_mask
    grad_first = grad_glu * gate_value
    grad_second = grad_glu * first_half * gate_value * (1.0 - gate_value)
    grad_pre = jnp.concatenate([grad_first, grad_second], 1).astype(jnp.bfloat16)[None]
    return (
        grad_pre,
        weight_shard / replicas,
        kernel_sum / replicas,
        sum_gain / replicas,
        sum_shift / replicas,
    )


def solution(mesh):
    return jax.shard_map(
        on_device,
        mesh=mesh,
        in_specs=(
            P(("dp", "local"), None, None),
            P(("dp", "local")),
            P(),
            P(),
            P(),
            P(),
            P(("dp", "local"), None, None),
        ),
        out_specs=(P(("dp", "local"), None, None), P("dp", "local"), P(), P(), P()),
        check_vma=False,
    )
```

profile of v0, /device:TPU:0, one launch (start us, length us, event | category | flops | bytes accessed | tf_op | source)
XLA Modules:
  0.0 228.4 jit_solution(6184416316779539486)
XLA Ops:
  7.2 0.0 reduce-scatter.3.cloned.1.call-start
  7.9 1.1 slice_reduce_fusion.4
  9.0 1.8 fusion.1
  10.8 0.0 copy-start.2
  10.8 0.0 copy-start.3
  10.8 1.1 multiply_reduce_fusion.7
  11.9 42.4 %all-reduce.3 = (f32[1536]{0:T(1024)S(1)}, f32[]{:T(128)}, f32[1536]{0:T(1024)S(1)}) all-reduce(f32[1536]{0:T(1024)S(1)} %get-tuple-element.11, f32[]{:T(128)S(6)} %convert_element_type.50, f32[1536]{0:T(1024)S(1)} %get-tuple-element.10), channel_id=1, replica_groups=mesh['dp'=16,'local'=2] {'dp','local'}, use_global_device_ids=true, to_apply=%region_4.5 | all-reduce | flops 3073 | bytes 24584 | tf_op jit(solution)/shard_map/psum | solution.py:24
  54.4 0.0 copy-done.2
  54.4 0.7 fusion.17
  55.0 0.7 add_rsqrt_fusion
  55.7 0.0 copy-done.3
  55.7 6.4 %fusion.7 = f32[1536,1536]{1,0:T(8,128)} fusion(f32[256,1536]{1,0:T(8,128)S(1)} %get-tuple-element.29, f32[1536]{0:T(1024)S(1)} %copy-done.3, f32[1536]{0:T(1024)S(1)} %add_rsqrt_fusion, f32[1536]{0:T(1024)S(1)} %get-tuple-element.28, f32[1536]{0:T(1024)S(1)} %copy-done.2, bf16[1,256,1536]{2,1,0:T(8,128)(2,1)} %param.13, bf16[256]{0:T(256)(128)(2,1)S(1)} %fusion.18), kind=kOutput, calls=%fused_computation.33 | convolution fusion | flops 1211891712 | bytes 11821568 | tf_op jit(solution)/shard_map/dot_general | solution.py:41
  62.1 0.0 reduce-scatter.3.cloned.1.call-update
  62.2 0.0 reduce-scatter.5.cloned.1.call-start
  62.2 5.6 %fusion.20 = (f32[1536]{0:T(1024)S(1)}, f32[1536]{0:T(1024)S(1)}, f32[256,1536]{1,0:T(8,128)}) fusion(f32[1536]{0:T(1024)S(1)} %add_rsqrt_fusion, f32[256,1536]{1,0:T(8,128)S(1)} %get-tuple-element.29, f32[1536]{0:T(1024)S(1)} %get-tuple-element.28, f32[1536]{0:T(1024)S(1)} %copy-done.3, f32[1536]{0:T(1024)S(1)} %copy-done.2, ...), kind=kOutput, calls=%fused_computation.60 | convolution fusion | flops 1214247936 | bytes 8688128 | tf_op jit(solution)/shard_map/dot_general | solution.py:44
  67.8 41.1 %all-reduce.2 = (f32[1536]{0:T(1024)S(1)}, f32[1536]{0:T(1024)S(1)}) all-reduce(f32[1536]{0:T(1024)S(1)} %get-tuple-element.13, f32[1536]{0:T(1024)S(1)} %get-tuple-element.12), channel_id=1, replica_groups=mesh['dp'=16,'local'=2] {'dp','local'}, use_global_device_ids=true, to_apply=%region_8.9 | all-reduce | flops 3072 | bytes 24576 | tf_op jit(solution)/shard_map/psum | solution.py:49
  108.9 0.0 copy-start
  108.9 3.5 %multiply_reduce_fusion = (f32[1536]{0:T(1024)S(1)}, f32[1536]{0:T(1024)S(1)}, f32[1536]{0:T(1024)S(1)}, f32[1536]{0:T(1024)S(1)}, f32[1536]{0:T(1024)S(1)}, /*index=5*/f32[256,1536]{1,0:T(8,128)S(1)}) fusion(f32[256,1536]{1,0:T(8,128)S(1)} %fusion.1, f32[256,1536]{1,0:T(8,128)} %get-tuple-element.30, f32[]{:T(128)} %get-tuple-element.22, ...), kind=kLoop, calls=%fused_computation.12 | loop fusion | flops 7070208 | bytes 6353924 | tf_op jit(solution)/shard_map/reduce_sum | solution.py:56
  112.4 0.0 copy-done
  112.4 0.0 copy-start.1
  112.4 2.2 fusion.8
  114.6 59.1 %reduce-scatter.3.cloned.1.call-done = f32[96,1536]{1,0:T(8,128)} async-done(((f32[1536,1536]{1,0:T(8,128)}), f32[96,1536]{1,0:T(8,128)}) %reduce-scatter.3.cloned.1.call-update) | async-done | bytes 589840 | tf_op jit(solution)/shard_map/reduce_scatter | solution.py:42
  173.7 0.0 reduce-scatter.5.cloned.1.call-update
  173.7 0.0 copy-done.1
  173.7 1.4 fusion.9
  175.2 0.1 stack.23
  175.2 40.7 %psum.47 = f32[5,1536]{1,0:T(8,128)S(1)} all-reduce(f32[5,1536]{1,0:T(8,128)S(1)} %stack.23), channel_id=1, replica_groups=mesh['dp'=16,'local'=2] {'dp','local'}, use_global_device_ids=true, to_apply=%region_16.17 | all-reduce | flops 7680 | bytes 61440 | tf_op jit(solution)/shard_map/psum | solution.py:58
  216.0 0.6 broadcast_multiply_fusion.2
  216.6 2.7 %pad_maximum_fusion = bf16[1,256,3072]{2,1,0:T(8,128)(2,1)} fusion(bf16[1,256,1536]{2,1,0:T(8,128)(2,1)} %fusion.9, bf16[1,256,1536]{2,1,0:T(8,128)(2,1)} %get-tuple-element.25), kind=kLoop, calls=%fused_computation.8 | loop fusion | flops 3145728 | bytes 3145728 | tf_op jit(solution)/shard_map/concatenate | solution.py:68
  219.2 0.6 broadcast_multiply_fusion.1
  219.9 0.0 reduce-scatter.5.cloned.1.call-done
  219.9 1.7 broadcast_multiply_fusion
  (7 shorter events, 0.0 us)
Async XLA Ops:
  7.2 166.5 %reduce-scatter.3.cloned.1.call-start = ((), (), s32[]{:S(2)}) async-start(), calls=%async_computation.2 | async-start | bytes 10027008 | tf_op jit(solution)/shard_map/reduce_scatter | solution.py:42
  10.8 43.6 %copy-start.2 = (f32[1536]{0:T(1024)S(1)}, f32[1536]{0:T(1024)}, u32[]{:S(2)}) copy-start(f32[1536]{0:T(1024)} %param.10) | copy-start | bytes 18436
  10.8 44.9 %copy-start.3 = (f32[1536]{0:T(1024)S(1)}, f32[1536]{0:T(1024)}, u32[]{:S(2)}) copy-start(f32[1536]{0:T(1024)} %param.11) | copy-start | bytes 18436
  62.2 157.7 %reduce-scatter.5.cloned.1.call-start = ((), (), s32[]{:S(2)}) async-start(), calls=%async_computation.3 | async-start | bytes 884736 | tf_op jit(solution)/shard_map/reduce_scatter | solution.py:43
  108.9 3.5 %copy-start = (bf16[1,256,3072]{2,1,0:T(8,128)(2,1)S(1)}, bf16[1,256,3072]{2,1,0:T(8,128)(2,1)}, u32[]{:S(2)}) copy-start(bf16[1,256,3072]{2,1,0:T(8,128)(2,1)} %param.7) | copy-start | bytes 4718596
  112.4 61.3 %copy-start.1 = (bf16[1,256,3072]{2,1,0:T(8,128)(2,1)S(1)}, bf16[1,256,3072]{2,1,0:T(8,128)(2,1)}, u32[]{:S(2)}) copy-start(bf16[1,256,3072]{2,1,0:T(8,128)(2,1)} %param.7) | copy-start | bytes 4718596
Sparse Core Ops, SparseCore 0:
  62.3 111.3 reduce-scatter.2
  175.9 15.2 reduce-scatter.4
where the time goes:
time: 229 us; the launch traced here: 228 us
  blocking collectives  124 us (54%)
  waiting for transfers between devices  59.1 us (26%)
  other arithmetic  16.9 us (7%)
  between operations  14.8 us (6%)
  matrix products  12 us (5%)
    reduce_scatter x1, waiting for transfers between devices, on_device(): lax.psum_scatter(wgrad_term, 'dp', scatter_dimension=0, tiled=True)  59.1 us
    psum x1, blocking collectives, on_device(): lax.psum((jnp.sum(conv_out * valid_mask, 0), jnp.sum(conv_out * conv_out...  42.4 us
    psum x1, blocking collectives, on_device(): lax.psum((jnp.sum(grad_act, 0), jnp.sum(grad_act * normed, 0)), ('dp', 'l...  41.1 us
    psum x1, blocking collectives, on_device(): kernel_sum = lax.psum(kernel_part, ('dp', 'local'))  40.7 us
    dot_general x1, matrix products, on_device(): lax.dot_general(swished, masked_cot, contract, preferred_element_type=jnp...  6.43 us
    concatenate x3, other arithmetic, on_device(): jnp.concatenate([grad_first, grad_second], 1).astype(jnp.bfloat16)[None]  6.24 us
    dot_general x1, matrix products, on_device(): lax.dot_general(masked_cot, w_out, (((1,), (1,)), ((), ())), preferred_el...  5.56 us
  transfers between devices with their start and end apart: 2, of which 1 were waited for; matrix products, arithmetic and copies ran while one was open for 7% of the time, Pallas kernels for 0%

commit v1 on v0

--- a/solution.py
+++ b/solution.py
@@ -55,7 +55,8 @@
     kernel_part = jnp.stack(
         [jnp.sum(grad_conv * padded[j : j + frames], 0) for j in range(kernel_taps)], 0
     )
-    kernel_sum = lax.psum(kernel_part, ("dp", "local"))
+    inner = lax.psum(kernel_part, "local")
+    kernel_sum = lax.psum(inner, "dp")
     grad_padded = jnp.pad(grad_conv, ((half_width, half_width), (0, 0)))
     grad_glu = kernel[0] * grad_padded[kernel_taps - 1 : kernel_taps - 1 + frames]
     for j in range(1, kernel_taps):

time: 229 us -> 255 us (1.11)
  blocking collectives: 124 us -> 150 us
    psum x1 -> x2, blocking collectives: 40.7 us -> 66.8 us  [the longest x1 57.7 us: on_device(): kernel_sum = lax.psum(inner, 'dp')]
where the time goes in v1:
time: 255 us
  blocking collectives  150 us (59%)
  waiting for transfers between devices  59.1 us (23%)
  other arithmetic  16.9 us (7%)
  between operations  14.8 us (6%)
  matrix products  12 us (5%)
    reduce_scatter x1, waiting for transfers between devices, on_device(): lax.psum_scatter(wgrad_term, 'dp', scatter_dimension=0, tiled=True)  59.1 us
    psum x1, blocking collectives, on_device(): kernel_sum = lax.psum(inner, 'dp')  57.7 us
    psum x1, blocking collectives, on_device(): lax.psum((jnp.sum(conv_out * valid_mask, 0), jnp.sum(conv_out * conv_out...  42.4 us
    psum x1, blocking collectives, on_device(): lax.psum((jnp.sum(grad_act, 0), jnp.sum(grad_act * normed, 0)), ('dp', 'l...  41.1 us
    psum x1, blocking collectives, on_device(): inner = lax.psum(kernel_part, 'local')  9.14 us
    dot_general x1, matrix products, on_device(): lax.dot_general(swished, masked_cot, contract, preferred_element_type=jnp...  6.43 us
    concatenate x3, other arithmetic, on_device(): jnp.concatenate([grad_first, grad_second], 1).astype(jnp.bfloat16)[None]  6.24 us
    dot_general x1, matrix products, on_device(): lax.dot_general(masked_cot, w_out, (((1,), (1,)), ((), ())), preferred_el...  5.56 us
  transfers between devices with their start and end apart: 2, of which 1 were waited for; matrix products, arithmetic and copies ran while one was open for 7% of the time, Pallas kernels for 0%

profile of v1, /device:TPU:0, one launch (start us, length us, event | category | flops | bytes accessed | tf_op | source)
XLA Modules:
  0.0 254.5 jit_solution(5717683161923721577)
XLA Ops:
  7.2 0.0 reduce-scatter.3.cloned.1.call-start
  7.9 1.1 slice_reduce_fusion.4
  9.0 1.8 fusion.1
  10.8 0.0 copy-start.2
  10.8 0.0 copy-start.3
  10.8 1.1 multiply_reduce_fusion.7
  11.9 42.4 %all-reduce.3 = (f32[1536]{0:T(1024)S(1)}, f32[]{:T(128)}, f32[1536]{0:T(1024)S(1)}) all-reduce(f32[1536]{0:T(1024)S(1)} %get-tuple-element.11, f32[]{:T(128)S(6)} %convert_element_type.50, f32[1536]{0:T(1024)S(1)} %get-tuple-element.10), channel_id=1, replica_groups=mesh['dp'=16,'local'=2] {'dp','local'}, use_global_device_ids=true, to_apply=%region_4.5 | all-reduce | flops 3073 | bytes 24584 | tf_op jit(solution)/shard_map/psum | solution.py:24
  54.4 0.0 copy-done.2
  54.4 0.7 fusion.17
  55.0 0.7 add_rsqrt_fusion
  55.7 0.0 copy-done.3
  55.7 6.4 %fusion.7 = f32[1536,1536]{1,0:T(8,128)} fusion(f32[256,1536]{1,0:T(8,128)S(1)} %get-tuple-element.29, f32[1536]{0:T(1024)S(1)} %copy-done.3, f32[1536]{0:T(1024)S(1)} %add_rsqrt_fusion, f32[1536]{0:T(1024)S(1)} %get-tuple-element.28, f32[1536]{0:T(1024)S(1)} %copy-done.2, bf16[1,256,1536]{2,1,0:T(8,128)(2,1)} %param.13, bf16[256]{0:T(256)(128)(2,1)S(1)} %fusion.18), kind=kOutput, calls=%fused_computation.33 | convolution fusion | flops 1211891712 | bytes 11821568 | tf_op jit(solution)/shard_map/dot_general | solution.py:41
  62.1 0.0 reduce-scatter.3.cloned.1.call-update
  62.2 0.0 reduce-scatter.5.cloned.1.call-start
  62.2 5.6 %fusion.20 = (f32[1536]{0:T(1024)S(1)}, f32[1536]{0:T(1024)S(1)}, f32[256,1536]{1,0:T(8,128)}) fusion(f32[1536]{0:T(1024)S(1)} %add_rsqrt_fusion, f32[256,1536]{1,0:T(8,128)S(1)} %get-tuple-element.29, f32[1536]{0:T(1024)S(1)} %get-tuple-element.28, f32[1536]{0:T(1024)S(1)} %copy-done.3, f32[1536]{0:T(1024)S(1)} %copy-done.2, ...), kind=kOutput, calls=%fused_computation.60 | convolution fusion | flops 1214247936 | bytes 8688128 | tf_op jit(solution)/shard_map/dot_general | solution.py:44
  67.8 41.1 %all-reduce.2 = (f32[1536]{0:T(1024)S(1)}, f32[1536]{0:T(1024)S(1)}) all-reduce(f32[1536]{0:T(1024)S(1)} %get-tuple-element.13, f32[1536]{0:T(1024)S(1)} %get-tuple-element.12), channel_id=1, replica_groups=mesh['dp'=16,'local'=2] {'dp','local'}, use_global_device_ids=true, to_apply=%region_8.9 | all-reduce | flops 3072 | bytes 24576 | tf_op jit(solution)/shard_map/psum | solution.py:49
  108.9 0.0 copy-start
  108.9 3.5 %multiply_reduce_fusion = (f32[1536]{0:T(1024)S(1)}, f32[1536]{0:T(1024)S(1)}, f32[1536]{0:T(1024)S(1)}, f32[1536]{0:T(1024)S(1)}, f32[1536]{0:T(1024)S(1)}, /*index=5*/f32[256,1536]{1,0:T(8,128)S(1)}) fusion(f32[256,1536]{1,0:T(8,128)S(1)} %fusion.1, f32[256,1536]{1,0:T(8,128)} %get-tuple-element.30, f32[]{:T(128)} %get-tuple-element.22, ...), kind=kLoop, calls=%fused_computation.12 | loop fusion | flops 7070208 | bytes 6353924 | tf_op jit(solution)/shard_map/reduce_sum | solution.py:56
  112.4 0.0 copy-done
  112.4 0.0 copy-start.1
  112.4 2.2 fusion.8
  114.6 59.1 %reduce-scatter.3.cloned.1.call-done = f32[96,1536]{1,0:T(8,128)} async-done(((f32[1536,1536]{1,0:T(8,128)}), f32[96,1536]{1,0:T(8,128)}) %reduce-scatter.3.cloned.1.call-update) | async-done | bytes 589840 | tf_op jit(solution)/shard_map/reduce_scatter | solution.py:42
  173.7 0.0 reduce-scatter.5.cloned.1.call-update
  173.7 0.0 copy-done.1
  173.7 1.4 fusion.9
  175.2 0.1 stack.23
  175.2 9.1 %psum.54 = f32[5,1536]{1,0:T(8,128)S(1)} all-reduce(f32[5,1536]{1,0:T(8,128)S(1)} %stack.23), channel_id=1, replica_groups=mesh['dp'=16,'local'=2] {'local'}, use_global_device_ids=true, to_apply=%region_16.17 | all-reduce | flops 7680 | bytes 61440 | tf_op jit(solution)/shard_map/psum | solution.py:58
  184.4 57.7 %psum.55 = f32[5,1536]{1,0:T(8,128)S(1)} all-reduce(f32[5,1536]{1,0:T(8,128)S(1)} %psum.54), channel_id=1, replica_groups=mesh['dp'=16,'local'=2] {'dp'}, use_global_device_ids=true, to_apply=%region_17.18 | all-reduce | flops 7680 | bytes 61440 | tf_op jit(solution)/shard_map/psum | solution.py:59
  242.1 0.6 broadcast_multiply_fusion.2
  242.7 2.7 %pad_maximum_fusion = bf16[1,256,3072]{2,1,0:T(8,128)(2,1)} fusion(bf16[1,256,1536]{2,1,0:T(8,128)(2,1)} %fusion.9, bf16[1,256,1536]{2,1,0:T(8,128)(2,1)} %get-tuple-element.25), kind=kLoop, calls=%fused_computation.8 | loop fusion | flops 3145728 | bytes 3145728 | tf_op jit(solution)/shard_map/concatenate | solution.py:69
  245.3 0.6 broadcast_multiply_fusion.1
  246.0 1.7 broadcast_multiply_fusion
  (8 shorter events, 0.0 us)
Async XLA Ops:
  7.2 166.5 %reduce-scatter.3.cloned.1.call-start = ((), (), s32[]{:S(2)}) async-start(), calls=%async_computation.2 | async-start | bytes 10027008 | tf_op jit(solution)/shard_map/reduce_scatter | solution.py:42
  10.8 43.6 %copy-start.2 = (f32[1536]{0:T(1024)S(1)}, f32[1536]{0:T(1024)}, u32[]{:S(2)}) copy-start(f32[1536]{0:T(1024)} %param.10) | copy-start | bytes 18436
  10.8 44.9 %copy-start.3 = (f32[1536]{0:T(1024)S(1)}, f32[1536]{0:T(1024)}, u32[]{:S(2)}) copy-start(f32[1536]{0:T(1024)} %param.11) | copy-start | bytes 18436
  62.2 183.8 %reduce-scatter.5.cloned.1.call-start = ((), (), s32[]{:S(2)}) async-start(), calls=%async_computation.3 | async-start | bytes 884736 | tf_op jit(solution)/shard_map/reduce_scatter | solution.py:43
  108.9 3.5 %copy-start = (bf16[1,256,3072]{2,1,0:T(8,128)(2,1)S(1)}, bf16[1,256,3072]{2,1,0:T(8,128)(2,1)}, u32[]{:S(2)}) copy-start(bf16[1,256,3072]{2,1,0:T(8,128)(2,1)} %param.7) | copy-start | bytes 4718596
  112.4 61.3 %copy-start.1 = (bf16[1,256,3072]{2,1,0:T(8,128)(2,1)S(1)}, bf16[1,256,3072]{2,1,0:T(8,128)(2,1)}, u32[]{:S(2)}) copy-start(bf16[1,256,3072]{2,1,0:T(8,128)(2,1)} %param.7) | copy-start | bytes 4718596
Sparse Core Ops, SparseCore 0:
  62.3 111.3 reduce-scatter.2
  175.9 15.2 reduce-scatter.4
